TPU v7x, 256 devices: a whole 4x4x8 slice. The times are simulated.
256 devices in a mesh: src: 64 (over x, z, core), grp: 4 (over y).
Axes of the slice: x: 4, y: 4, z: 8, core: 2. Of those that a mesh axis runs over, the one named last changes fastest.
Arguments:
- currents: bfloat16 [524288, 1024], P(('src', 'grp')), may hold values from -6 to 6
- leaf_basis: bfloat16 [2, 40, 524288], P(None, None, ('src', 'grp')), may hold values from -6 to 6
- leaf_box: int32 [524288], P(('src', 'grp')), may hold values from 0 to 7, as said below
- box_count: int32 [2048], P(('src', 'grp')), may hold values from 1 to 2041, as said below
- merge_factor: bfloat16 [2, 2560, 81920], P(None, None, ('src', 'grp')), may hold values from -0.25 to 0.25
- angle_factor: bfloat16 [4096, 4, 2, 2560], P('src'), may hold values from -0.0390625 to 0.0390625
Outputs:
- normalized: float32 [4096, 512], P('src', 'grp')
- peak_value: float32 [512], P('grp')
Inputs may be any that keep to these rules, and one draw needn't show every extreme that they name: `leaf_box`: every source block of 2048 currents holds one or more currents of each of its 8 leaf boxes; some blocks put all but 7 of their currents into one box. box_count[k * 8 + b] is the number of currents of source block k whose leaf_box is b.
All inputs are finite; a program needn't handle non-finite values.
Results may differ from a plain program's by a relative error of at most 0.0057.
Values may be sent and summed in bfloat16 or wider, within the bound.
A program may use at most 128 MiB of HBM per device.

v0:
```python
import functools

import jax
import jax.numpy as jnp
from jax import lax
from jax.experimental import pallas as pl
from jax.experimental.pallas import tpu as pltpu
from jax.sharding import PartitionSpec as P

MESH = pl.DeviceIdType.MESH
BF = jnp.bfloat16
F32 = jnp.float32

NX, NY, NZ, NC = 4, 4, 8, 2
CHIPS = NX * NZ
R = 40
LEAF = 8
S_DEV = 2048
NE = 512
A = 64
EQ = NE // NY
LR = LEAF * R
GX = NZ * NC * R


def tdot(a, b):
    return lax.dot_general(a, b, (((0,), (0,)), ((), ())), preferred_element_type=F32)


def dot(a, b):
    return jnp.dot(a, b, preferred_element_type=F32)


def kernel(
    cnt,
    box,
    x_hbm,
    basis_hbm,
    mt_hbm,
    own_hbm,
    inten,
    top_out,
    xv,
    basis,
    mt,
    own,
    ft,
    lmat,
    mm,
    rhs,
    bb,
    rf,
    pa,
    pb,
    ta1,
    tb1,
    ta2,
    tb2,
    ra1,
    rb1,
    ra2,
    rb2,
    qa,
    qb,
    ta3,
    tb3,
    ta4,
    tb4,
    ra3,
    rb3,
    ra4,
    rb4,
    sm,
    rz,
    last32,
    mx,
    m1,
    mz,
    m2,
    ld_sem,
    fs_sem,
    fr_sem,
    ps_sem,
    pr_sem,
    s1,
    r1,
    s2,
    r2,
    zs,
    zr,
    ms,
    mr,
):
    src = lax.axis_index("src")
    y = lax.axis_index("grp")
    c = lax.rem(src, NC)
    z = lax.rem(src // NC, NZ)
    x = src // (NC * NZ)
    chip = src // NC
    mm4 = mm.reshape(NX, NZ, NC * R, 2 * LR)
    ft3 = ft.reshape(CHIPS, NC * R, 2 * A)

    def dev(xx, yy, zz, cc):
        return ((xx * NZ + zz) * NC + cc, yy)

    def remote(a, b, send, recv, to):
        return lambda: pltpu.make_async_remote_copy(
            src_ref=a,
            dst_ref=b,
            send_sem=send,
            recv_sem=recv,
            device_id=to,
            device_id_type=MESH,
        )

    def target_z(k):
        even = (1 - lax.rem(k, 2)) * (k // 2 + 1)
        odd = lax.rem(k, 2) * ((k + 1) // 2 + (k // (NZ - 1)) * (NZ // 2))
        return lax.rem(z + NZ + even - odd, NZ)

    xp, xm, xo = lax.rem(x + 1, NX), lax.rem(x + 3, NX), lax.rem(x + 2, NX)
    yp, ym, yo = lax.rem(y + 1, NY), lax.rem(y + 3, NY), lax.rem(y + 2, NY)
    to_xp, to_xm = dev(xp, y, z, c), dev(xm, y, z, c)
    to_yp, to_ym = dev(x, yp, z, c), dev(x, ym, z, c)
    to_sib = dev(x, y, z, 1 - c)

    loads = [
        pltpu.make_async_copy(a, b, ld_sem.at[i])
        for i, (a, b) in enumerate(
            [(basis_hbm, basis), (mt_hbm, mt), (own_hbm, own), (x_hbm, xv)]
        )
    ]
    for copy in loads:
        copy.start()

    barrier = pltpu.get_barrier_semaphore()

    def greet(i, carry):
        other = lax.rem(chip + i, CHIPS)
        pl.semaphore_signal(
            barrier, inc=1, device_id=(other * NC + c, y), device_id_type=MESH
        )
        return carry

    lax.fori_loop(1, CHIPS, greet, 0)
    greeted = [to_yp, to_ym] + [dev(lax.rem(x + d, NX), y, z, 1 - c) for d in range(NX)]
    for to in greeted:
        pl.semaphore_signal(barrier, inc=1, device_id=to, device_id_type=MESH)

    with jax.named_scope("build"):
        loads[0].wait()
        scale = [
            lax.rsqrt(jnp.full((8, 128), cnt[b], jnp.int32).astype(F32))[0:1, 0:1]
            for b in range(LEAF)
        ]
        width = 256

        def build(i, carry):
            cols = pl.ds(pl.multiple_of(i * width, width), width)
            where = box[:, cols]
            gains = [
                jnp.where(where == b, jnp.broadcast_to(scale[b], (1, width)), 0.0)
                for b in range(LEAF)
            ]
            for p in range(2):
                wide = basis[p, :, cols].astype(F32)
                rows = jnp.concatenate([wide * g for g in gains], axis=0)
                lmat[p * LR : (p + 1) * LR, cols] = rows.astype(BF)
            return carry

        lax.fori_loop(0, S_DEV // width, build, 0)

    with jax.named_scope("turn"):
        loads[1].wait()

        def turn(i, carry):
            span = pl.ds(pl.multiple_of(i * 128, 128), 128)
            mm[span, :] = jnp.transpose(mt[:, span])
            return carry

        lax.fori_loop(0, NX * GX // 128, turn, 0)

    with jax.named_scope("turn_f"):
        loads[2].wait()

        def turn_f(i, carry):
            span = pl.ds(pl.multiple_of(i * 128, 128), 128)
            ft[span, :] = jnp.transpose(own[:, span])
            return carry

        lax.fori_loop(0, NX * GX // 128, turn_f, 0)
        rf[chip] = ft3[chip]

    with jax.named_scope("barrier"):
        pl.semaphore_wait(barrier, CHIPS - 1 + len(greeted))

    def f_copy(i):
        k, dx = i // NX, lax.rem(i, NX)
        tx, tz = lax.rem(x + dx, NX), target_z(k)
        return remote(
            ft3.at[tx * NZ + tz], rf.at[chip], fs_sem.at[i], fr_sem.at[chip], dev(tx, y, tz, c)
        )()

    def f_send(i, carry):
        f_copy(i).start()
        return carry

    with jax.named_scope("f_send"):
        lax.fori_loop(0, CHIPS - NX, f_send, 0)
        lax.fori_loop(CHIPS - NX + 1, CHIPS, f_send, 0)

    tile = 256
    with jax.named_scope("leaf"):
        loads[3].wait()

        def leaf(i, carry):
            lo = pl.ds(pl.multiple_of(i * tile, tile), tile)
            hi = pl.ds(pl.multiple_of(NE + i * tile, tile), tile)
            u = dot(lmat[...], xv[:, lo])
            w = dot(lmat[...], xv[:, hi])
            real = (u[:LR] - w[LR:]).astype(BF)
            imag = (w[:LR] + u[LR:]).astype(BF)
            rhs[:LR, lo] = real
            rhs[LR:, hi] = real
            rhs[:LR, hi] = imag
            rhs[LR:, lo] = -imag
            return carry

        lax.fori_loop(0, NE // tile, leaf, 0)

    def pair_copy(k):
        return remote(bb.at[k, :, 2], bb.at[k, :, c], ps_sem.at[k], pr_sem.at[k], to_sib)()

    def first_copies(k):
        return [
            remote(ta1.at[k, 0:2], ra1.at[k, 0], s1.at[k, 0], r1.at[k, 0], to_xp),
            remote(tb1.at[k, 0:2], rb1.at[k, 0], s1.at[k, 1], r1.at[k, 1], to_yp),
            remote(ta1.at[k, 2:4], ra1.at[k, 1], s1.at[k, 2], r1.at[k, 2], to_xm),
            remote(tb1.at[k, 2:4], rb1.at[k, 1], s1.at[k, 3], r1.at[k, 3], to_ym),
        ]

    def second_copies(k):
        return [
            remote(ta2.at[k, 0], ra2.at[k, 0], s1.at[k, 4], r1.at[k, 4], to_xp),
            remote(tb2.at[k, 0], rb2.at[k, 0], s1.at[k, 5], r1.at[k, 5], to_yp),
            remote(ta2.at[k, 1], ra2.at[k, 1], s1.at[k, 6], r1.at[k, 6], to_xm),
            remote(tb2.at[k, 1], rb2.at[k, 1], s1.at[k, 7], r1.at[k, 7], to_ym),
        ]

    def third_copies(k):
        return [
            remote(ta3.at[k, 0:32], ra3.at[k, 0], s2.at[k, 0], r2.at[k, 0], to_yp),
            remote(tb3.at[k, 0:32], rb3.at[k, 0], s2.at[k, 1], r2.at[k, 1], to_xp),
            remote(ta3.at[k, 32:64], ra3.at[k, 1], s2.at[k, 2], r2.at[k, 2], to_ym),
            remote(tb3.at[k, 32:64], rb3.at[k, 1], s2.at[k, 3], r2.at[k, 3], to_xm),
        ]

    def fourth_copies(k):
        return [
            remote(ta4.at[k, 0], ra4.at[k, 0], s2.at[k, 4], r2.at[k, 4], to_yp),
            remote(tb4.at[k, 0], rb4.at[k, 0], s2.at[k, 5], r2.at[k, 5], to_xp),
            remote(ta4.at[k, 1], ra4.at[k, 1], s2.at[k, 6], r2.at[k, 6], to_ym),
            remote(tb4.at[k, 1], rb4.at[k, 1], s2.at[k, 7], r2.at[k, 7], to_xm),
        ]

    def z_copy(k):
        return remote(sm.at[k], rz.at[k], zs.at[k], zr.at[k], dev(x, y, target_z(k), c))()

    def stage_merge(k):
        left = mm4[:, target_z(k)].reshape(NX * NC * R, 2 * LR)
        for n in range(2 * NE // tile):
            cols = slice(n * tile, (n + 1) * tile)
            v = dot(left, rhs[:, cols])
            for i in range(NX):
                bb[k, i, 2 * c, :, cols] = v[2 * i * R : (2 * i + 1) * R].astype(BF)
                bb[k, i, 2 - c, :, cols] = v[(2 * i + 1) * R : (2 * i + 2) * R].astype(BF)
        pair_copy(k).start()

    def stage_patterns(k):
        tz = target_z(k)

        def arrived(i, carry):
            at = i * NZ + tz

            @pl.when(at != chip)
            def _():
                remote(ft3.at[0], rf.at[at], fs_sem.at[0], fr_sem.at[at], to_sib)().wait_recv()

            return carry

        lax.fori_loop(0, NX, arrived, 0)
        pair_copy(k).wait_recv()
        for i in range(NX):
            q = tdot(rf[i * NZ + tz], bb[k, i, 0:2].reshape(NC * R, 2 * NE))
            real = q[:A, :NE] - q[A:, NE:]
            imag = q[:A, NE:] + q[A:, :NE]
            for j in range(NY):
                pa[k, i, j] = real[:, j * EQ : (j + 1) * EQ]
                pb[k, j, i] = imag[:, j * EQ : (j + 1) * EQ]
        ta1[k] = pa[k, xo].astype(BF)
        tb1[k] = pb[k, yo].astype(BF)
        for copy in first_copies(k):
            copy().start()

    def stage_second(k):
        firsts, seconds = first_copies(k), second_copies(k)
        for n, (p, t, r, to, half) in enumerate(
            [
                (pa, ta2, ra1, xp, 0),
                (pb, tb2, rb1, yp, 0),
                (pa, ta2, ra1, xm, 1),
                (pb, tb2, rb1, ym, 1),
            ]
        ):
            mine, rest = (slice(0, 2), slice(2, 4)) if half == 0 else (slice(2, 4), slice(0, 2))
            t[k, half, rest] = p[k, to, rest].astype(BF)
            firsts[n]().wait_recv()
            t[k, half, mine] = (p[k, to, mine] + r[k, half].astype(F32)).astype(BF)
            seconds[n]().start()

    def stage_third(k):
        seconds, thirds = second_copies(k), third_copies(k)
        for n, (p, q, t, r, me, to) in enumerate(
            [(pa, qa, ta3, ra2, x, yo), (pb, qb, tb3, rb2, y, xo)]
        ):
            seconds[n]().wait_recv()
            seconds[n + 2]().wait_recv()
            q[k] = p[k, me] + r[k, 0].astype(F32) + r[k, 1].astype(F32)
            t[k] = q[k, to].astype(BF)
            thirds[n]().start()
            thirds[n + 2]().start()

    def stage_fourth(k):
        thirds, fourths = third_copies(k), fourth_copies(k)
        for n, (q, t, r, to, half) in enumerate(
            [
                (qa, ta4, ra3, yp, 0),
                (qb, tb4, rb3, xp, 0),
                (qa, ta4, ra3, ym, 1),
                (qb, tb4, rb3, xm, 1),
            ]
        ):
            mine, rest = (slice(0, 32), slice(32, 64)) if half == 0 else (slice(32, 64), slice(0, 32))
            t[k, half, rest] = q[k, to, rest].astype(BF)
            thirds[n]().wait_recv()
            t[k, half, mine] = (q[k, to, mine] + r[k, half].astype(F32)).astype(BF)
            fourths[n]().start()

    def stage_last(k):
        for copy in fourth_copies(k):
            copy().wait_recv()
        real = qa[k, y] + ra4[k, 0].astype(F32) + ra4[k, 1].astype(F32)
        imag = qb[k, x] + rb4[k, 0].astype(F32) + rb4[k, 1].astype(F32)
        last32[0:A] = real
        last32[A:] = imag

        @pl.when(k < NZ - 1)
        def _():
            sm[k, 0:A] = real.astype(BF)
            sm[k, A:] = imag.astype(BF)
            z_copy(k).start()

    stages = [
        (stage_merge, 0),
        (stage_patterns, 1),
        (stage_second, 2),
        (stage_third, 4),
        (stage_fourth, 6),
        (stage_last, 8),
    ]

    def flow(t, carry):
        for stage, lag in stages:

            @pl.when(jnp.logical_and(t >= lag, t < NZ + lag))
            def _(stage=stage, lag=lag):
                with jax.named_scope(stage.__name__):
                    stage(t - lag)

        return carry

    lax.fori_loop(0, NZ + stages[-1][1], flow, 0)

    total = last32[...]
    with jax.named_scope("z_wait"):
        for k in range(NZ - 1):
            z_copy(k).wait_recv()
            total = total + rz[k].astype(F32)
    intensity = total[:A] * total[:A] + total[A:] * total[A:]
    inten[...] = intensity
    mx[...] = jnp.max(intensity, axis=0, keepdims=True)

    slot = x * NC + c
    m1[slot] = mx[...]

    def near(i, sender):
        other = lax.rem(slot + i, NX * NC)
        at = slot if sender else other
        to = dev(other // NC, y, z, lax.rem(other, NC))
        return remote(mx, m1.at[at], ms.at[i], mr.at[at], to)()

    for i in range(1, NX * NC):
        near(i, True).start()
    with jax.named_scope("near_wait"):
        for i in range(1, NX * NC):
            near(i, False).wait_recv()
    mz[...] = jnp.max(m1[...], axis=0)
    m2[z] = mz[...]

    def far(i, sender):
        oz = lax.rem(z + i, NZ)
        at = z if sender else oz
        return remote(mz, m2.at[at], ms.at[NZ + i], mr.at[NZ + at], dev(x, y, oz, c))()

    for i in range(1, NZ):
        far(i, True).start()
    with jax.named_scope("far_wait"):
        for i in range(1, NZ):
            far(i, False).wait_recv()
    top_out[...] = jnp.max(m2[...], axis=0)

    def drain_f(i, carry):
        f_copy(i).wait_send()
        return carry

    def drain(k, carry):
        pair_copy(k).wait_send()
        for copies in (first_copies(k), second_copies(k), third_copies(k), fourth_copies(k)):
            for copy in copies:
                copy().wait_send()

        @pl.when(k < NZ - 1)
        def _():
            z_copy(k).wait_send()
            near(k + 1, True).wait_send()
            far(k + 1, True).wait_send()

        return carry

    with jax.named_scope("drain"):
        lax.fori_loop(0, CHIPS - NX, drain_f, 0)
        lax.fori_loop(CHIPS - NX + 1, CHIPS, drain_f, 0)
        lax.fori_loop(0, NZ, drain, 0)


def finish(inten, top, out, peak):
    peak[...] = top[...]
    out[...] = inten[...] / (top[...] + 1.0)


def body(currents, leaf_basis, leaf_box, box_count, merge_factor, angle_factor):
    own = lax.dynamic_index_in_dim(angle_factor, lax.axis_index("grp"), 1, keepdims=False)
    own = jnp.transpose(own, (1, 0, 2)).reshape(2 * A, NX * GX)
    turned = jnp.transpose(merge_factor, (0, 2, 1)).reshape(2 * LR, NX * GX)

    vm = pltpu.VMEM
    dma = pltpu.SemaphoreType.DMA
    anyspace = pl.BlockSpec(memory_space=pl.ANY)
    invm = pl.BlockSpec(memory_space=pltpu.VMEM)
    shapes = (
        jax.ShapeDtypeStruct((A, EQ), F32),
        jax.ShapeDtypeStruct((1, EQ), F32),
    )
    inten, top = pl.pallas_call(
        kernel,
        out_shape=shapes,
        in_specs=[
            pl.BlockSpec(memory_space=pltpu.SMEM),
            invm,
            anyspace,
            anyspace,
            anyspace,
            anyspace,
        ],
        out_specs=(invm, invm),
        scratch_shapes=[
            vm((S_DEV, 2 * NE), BF),
            vm((2, R, S_DEV), BF),
            vm((2 * LR, NX * GX), BF),
            vm((2 * A, NX * GX), BF),
            vm((NX * GX, 2 * A), BF),
            vm((2 * LR, S_DEV), BF),
            vm((NX * GX, 2 * LR), BF),
            vm((2 * LR, 2 * NE), BF),
            vm((NZ, NX, 3, R, 2 * NE), BF),
            vm((CHIPS, NC * R, 2 * A), BF),
            vm((NZ, NX, NY, A, EQ), F32),
            vm((NZ, NY, NX, A, EQ), F32),
            vm((NZ, 4, A, EQ), BF),
            vm((NZ, 4, A, EQ), BF),
            vm((NZ, 2, 4, A, EQ), BF),
            vm((NZ, 2, 4, A, EQ), BF),
            vm((NZ, 2, 2, A, EQ), BF),
            vm((NZ, 2, 2, A, EQ), BF),
            vm((NZ, 2, 4, A, EQ), BF),
            vm((NZ, 2, 4, A, EQ), BF),
            vm((NZ, NY, A, EQ), F32),
            vm((NZ, NX, A, EQ), F32),
            vm((NZ, A, EQ), BF),
            vm((NZ, A, EQ), BF),
            vm((NZ, 2, A, EQ), BF),
            vm((NZ, 2, A, EQ), BF),
            vm((NZ, 2, A // 2, EQ), BF),
            vm((NZ, 2, A // 2, EQ), BF),
            vm((NZ, 2, A, EQ), BF),
            vm((NZ, 2, A, EQ), BF),
            vm((NZ, 2 * A, EQ), BF),
            vm((NZ, 2 * A, EQ), BF),
            vm((2 * A, EQ), F32),
            vm((1, EQ), F32),
            vm((NX * NC, 1, EQ), F32),
            vm((1, EQ), F32),
            vm((NZ, 1, EQ), F32),
            dma((4,)),
            dma((CHIPS,)),
            dma((CHIPS,)),
            dma((NZ,)),
            dma((NZ,)),
            dma((NZ, 8)),
            dma((NZ, 8)),
            dma((NZ, 8)),
            dma((NZ, 8)),
            dma((NZ,)),
            dma((NZ,)),
            dma((2 * NZ,)),
            dma((2 * NZ,)),
        ],
        compiler_params=pltpu.CompilerParams(
            collective_id=0, has_side_effects=True, vmem_limit_bytes=62 * 1024 * 1024
        ),
    )(
        box_count,
        leaf_box.reshape(1, S_DEV),
        currents,
        leaf_basis,
        turned,
        own,
    )
    normalized, peak = pl.pallas_call(
        finish,
        out_shape=shapes,
        in_specs=[invm, invm],
        out_specs=(invm, invm),
    )(inten, top)
    return normalized, peak.reshape(EQ)


def solution(mesh):
    in_specs = (
        P(("src", "grp"), None),
        P(None, None, ("src", "grp")),
        P(("src", "grp")),
        P(("src", "grp")),
        P(None, None, ("src", "grp")),
        P("src", None, None, None),
    )
    out_specs = (P("src", "grp"), P("grp"))
    return jax.shard_map(body, mesh=mesh, in_specs=in_specs, out_specs=out_specs, check_vma=False)
```

profile of v0, /device:TPU:1, one launch (start us, length us, event | category | flops | bytes accessed | tf_op | source)
XLA Modules:
  0.0 72.3 jit_solution(17099620813199101595)
XLA Ops:
  0.6 1.5 %constant_dynamic-slice_fusion = bf16[64,1,2,2560]{3,2,1,0:T(2,128)(2,1)S(1)} fusion(bf16[64,4,2,2560]{3,2,1,0:T(2,128)(2,1)} %param.11, s32[]{:T(128)S(6)} %select_n.4), kind=kLoop, calls=%fused_computation | loop fusion | bytes 1310724 | tf_op jit(solution)/shard_map/jit(dynamic_index_in_dim)/dynamic_slice | solution.py:452
  2.2 0.9 %copy.9 = bf16[64,1,2,2560]{3,0,2,1:T(8,128)(2,1)} copy(bf16[64,1,2,2560]{3,2,1,0:T(2,128)(2,1)S(1)} %constant_dynamic-slice_fusion) | data formatting | bytes 1310720
  3.1 67.9 %shard_map.77 = (f32[64,128]{1,0:T(8,128)}, f32[1,128]{1,0:T(1,128)}) custom-call(s32[8]{0:T(128)} %cnt.1, s32[1,2048]{1,0:T(1,128)} %bitcast.12, bf16[2048,1024]{1,0:T(8,128)(2,1)} %x_hbm.1, bf16[2,40,2048]{2,1,0:T(8,128)(2,1)} %basis_hbm.1, bf16[640,2560]{1,0:T(8,128)(2,1)} %bitcast.10, bf16[128,2560]{1,0:T(8,128)(2,1)} %bitcast.11), custom_call_target="tpu_custom_call" | custom-call | tf_op jit(solution)/shard_map/pallas_call | solution.py:464
  71.0 1.4 %shard_map.78 = (f32[64,128]{1,0:T(8,128)}, f32[1,128]{1,0:T(1,128)}) custom-call(f32[64,128]{1,0:T(8,128)} %get-tuple-element.6.inten, f32[1,128]{1,0:T(1,128)} %get-tuple-element.7.top), custom_call_target="tpu_custom_call" | custom-call | tf_op jit(solution)/shard_map/pallas_call | solution.py:539
where the time goes:
time: 72.6 us; the launch traced here: 72.3 us
  Pallas kernels  69.3 us (95%)
  local copies, waits for them, and re-layouts  2.45 us (3%)
    pallas_call x1, Pallas kernels, body(): pl.pallas_call(kernel, out_shape=shapes, in_specs=[pl.BlockSpec(memory_sp...  67.9 us
    dynamic_slice x1, local copies, waits for them, and re-layouts, body(): lax.dynamic_index_in_dim(angle_factor, lax.axis_index('grp'), 1, keepdims...  1.54 us

commit v1 on v0

--- a/solution.py
+++ b/solution.py
@@ -21,6 +21,10 @@
 EQ = NE // NY
 LR = LEAF * R
 GX = NZ * NC * R
+OFFSETS = (1, 7, 2, 6, 4, 3, 5, 0)
+LAGS = (0, 1, 3, 6, 8)
+AR = 64
+BR = 2 * A - AR
 
 
 def tdot(a, b):
@@ -62,17 +66,12 @@
     rb2,
     qa,
     qb,
-    ta3,
-    tb3,
-    ta4,
-    tb4,
-    ra3,
-    rb3,
-    ra4,
-    rb4,
     sm,
     rz,
-    last32,
+    tda,
+    tdb,
+    rda,
+    rdb,
     mx,
     m1,
     mz,
@@ -84,10 +83,10 @@
     pr_sem,
     s1,
     r1,
-    s2,
-    r2,
     zs,
     zr,
+    ds,
+    dr,
     ms,
     mr,
 ):
@@ -114,9 +113,10 @@
         )
 
     def target_z(k):
-        even = (1 - lax.rem(k, 2)) * (k // 2 + 1)
-        odd = lax.rem(k, 2) * ((k + 1) // 2 + (k // (NZ - 1)) * (NZ // 2))
-        return lax.rem(z + NZ + even - odd, NZ)
+        if isinstance(k, int):
+            return lax.rem(z + OFFSETS[k], NZ)
+        packed = jnp.int32(sum(o * NZ**i for i, o in enumerate(OFFSETS)))
+        return lax.rem(z + lax.rem(lax.shift_right_logical(packed, 3 * k), NZ), NZ)
 
     xp, xm, xo = lax.rem(x + 1, NX), lax.rem(x + 3, NX), lax.rem(x + 2, NX)
     yp, ym, yo = lax.rem(y + 1, NY), lax.rem(y + 3, NY), lax.rem(y + 2, NY)
@@ -127,7 +127,7 @@
     loads = [
         pltpu.make_async_copy(a, b, ld_sem.at[i])
         for i, (a, b) in enumerate(
-            [(basis_hbm, basis), (mt_hbm, mt), (own_hbm, own), (x_hbm, xv)]
+            [(own_hbm, own), (basis_hbm, basis), (x_hbm, xv), (mt_hbm, mt)]
         )
     ]
     for copy in loads:
@@ -143,12 +143,12 @@
         return carry
 
     lax.fori_loop(1, CHIPS, greet, 0)
-    greeted = [to_yp, to_ym] + [dev(lax.rem(x + d, NX), y, z, 1 - c) for d in range(NX)]
+    greeted = [to_yp, to_ym, dev(x, yo, z, c), to_sib]
     for to in greeted:
         pl.semaphore_signal(barrier, inc=1, device_id=to, device_id_type=MESH)
 
     with jax.named_scope("build"):
-        loads[0].wait()
+        loads[1].wait()
         scale = [
             lax.rsqrt(jnp.full((8, 128), cnt[b], jnp.int32).astype(F32))[0:1, 0:1]
             for b in range(LEAF)
@@ -170,50 +170,39 @@
 
         lax.fori_loop(0, S_DEV // width, build, 0)
 
-    with jax.named_scope("turn"):
-        loads[1].wait()
-
-        def turn(i, carry):
-            span = pl.ds(pl.multiple_of(i * 128, 128), 128)
-            mm[span, :] = jnp.transpose(mt[:, span])
-            return carry
-
-        lax.fori_loop(0, NX * GX // 128, turn, 0)
-
     with jax.named_scope("turn_f"):
-        loads[2].wait()
-
-        def turn_f(i, carry):
-            span = pl.ds(pl.multiple_of(i * 128, 128), 128)
+        loads[0].wait()
+
+        for i in range(NX * GX // 128):
+            span = slice(i * 128, (i + 1) * 128)
             ft[span, :] = jnp.transpose(own[:, span])
-            return carry
-
-        lax.fori_loop(0, NX * GX // 128, turn_f, 0)
         rf[chip] = ft3[chip]
 
     with jax.named_scope("barrier"):
         pl.semaphore_wait(barrier, CHIPS - 1 + len(greeted))
 
     def f_copy(i):
-        k, dx = i // NX, lax.rem(i, NX)
-        tx, tz = lax.rem(x + dx, NX), target_z(k)
+        k, dx = i // NX, i % NX
+        tx, tz = lax.rem(x + dx, NX), lax.rem(z + NZ - OFFSETS[k], NZ)
         return remote(
             ft3.at[tx * NZ + tz], rf.at[chip], fs_sem.at[i], fr_sem.at[chip], dev(tx, y, tz, c)
         )()
 
-    def f_send(i, carry):
-        f_copy(i).start()
-        return carry
-
     with jax.named_scope("f_send"):
-        lax.fori_loop(0, CHIPS - NX, f_send, 0)
-        lax.fori_loop(CHIPS - NX + 1, CHIPS, f_send, 0)
+        for i in range(CHIPS):
+            if i != CHIPS - NX:
+                f_copy(i).start()
 
     tile = 256
     with jax.named_scope("leaf"):
+        loads[2].wait()
         loads[3].wait()
+        turns = NX * GX // 128 // (NE // tile)
 
         def leaf(i, carry):
+            for n in range(turns):
+                span = pl.ds(pl.multiple_of((i * turns + n) * 128, 128), 128)
+                mm[span, :] = jnp.transpose(mt[:, span])
             lo = pl.ds(pl.multiple_of(i * tile, tile), tile)
             hi = pl.ds(pl.multiple_of(NE + i * tile, tile), tile)
             u = dot(lmat[...], xv[:, lo])
@@ -247,20 +236,24 @@
             remote(tb2.at[k, 1], rb2.at[k, 1], s1.at[k, 7], r1.at[k, 7], to_ym),
         ]
 
-    def third_copies(k):
+    def direct_copies(k, d, sender):
+        oy, ox = lax.rem(y + d, NY), lax.rem(x + d, NX)
+        ty, tx = (y, x) if sender else (oy, ox)
         return [
-            remote(ta3.at[k, 0:32], ra3.at[k, 0], s2.at[k, 0], r2.at[k, 0], to_yp),
-            remote(tb3.at[k, 0:32], rb3.at[k, 0], s2.at[k, 1], r2.at[k, 1], to_xp),
-            remote(ta3.at[k, 32:64], ra3.at[k, 1], s2.at[k, 2], r2.at[k, 2], to_ym),
-            remote(tb3.at[k, 32:64], rb3.at[k, 1], s2.at[k, 3], r2.at[k, 3], to_xm),
-        ]
-
-    def fourth_copies(k):
-        return [
-            remote(ta4.at[k, 0], ra4.at[k, 0], s2.at[k, 4], r2.at[k, 4], to_yp),
-            remote(tb4.at[k, 0], rb4.at[k, 0], s2.at[k, 5], r2.at[k, 5], to_xp),
-            remote(ta4.at[k, 1], ra4.at[k, 1], s2.at[k, 6], r2.at[k, 6], to_ym),
-            remote(tb4.at[k, 1], rb4.at[k, 1], s2.at[k, 7], r2.at[k, 7], to_xm),
+            remote(
+                tda.at[k, oy],
+                rda.at[k, ty],
+                ds.at[k, d],
+                dr.at[k, ty],
+                dev(x, oy, z, c),
+            ),
+            remote(
+                tdb.at[k, ox],
+                rdb.at[k, tx],
+                ds.at[k, NY + d],
+                dr.at[k, NY + tx],
+                dev(ox, y, z, c),
+            ),
         ]
 
     def z_copy(k):
@@ -295,8 +288,10 @@
             real = q[:A, :NE] - q[A:, NE:]
             imag = q[:A, NE:] + q[A:, :NE]
             for j in range(NY):
-                pa[k, i, j] = real[:, j * EQ : (j + 1) * EQ]
-                pb[k, j, i] = imag[:, j * EQ : (j + 1) * EQ]
+                pa[k, i, j] = real[:AR, j * EQ : (j + 1) * EQ]
+                if AR < A:
+                    pb[k, j, i, 0 : A - AR] = real[AR:, j * EQ : (j + 1) * EQ]
+                pb[k, j, i, A - AR :] = imag[:, j * EQ : (j + 1) * EQ]
         ta1[k] = pa[k, xo].astype(BF)
         tb1[k] = pb[k, yo].astype(BF)
         for copy in first_copies(k):
@@ -319,69 +314,53 @@
             seconds[n]().start()
 
     def stage_third(k):
-        seconds, thirds = second_copies(k), third_copies(k)
-        for n, (p, q, t, r, me, to) in enumerate(
-            [(pa, qa, ta3, ra2, x, yo), (pb, qb, tb3, rb2, y, xo)]
-        ):
+        seconds = second_copies(k)
+        for n, (p, q, t, r, me) in enumerate([(pa, qa, tda, ra2, x), (pb, qb, tdb, rb2, y)]):
             seconds[n]().wait_recv()
             seconds[n + 2]().wait_recv()
             q[k] = p[k, me] + r[k, 0].astype(F32) + r[k, 1].astype(F32)
-            t[k] = q[k, to].astype(BF)
-            thirds[n]().start()
-            thirds[n + 2]().start()
-
-    def stage_fourth(k):
-        thirds, fourths = third_copies(k), fourth_copies(k)
-        for n, (q, t, r, to, half) in enumerate(
-            [
-                (qa, ta4, ra3, yp, 0),
-                (qb, tb4, rb3, xp, 0),
-                (qa, ta4, ra3, ym, 1),
-                (qb, tb4, rb3, xm, 1),
-            ]
-        ):
-            mine, rest = (slice(0, 32), slice(32, 64)) if half == 0 else (slice(32, 64), slice(0, 32))
-            t[k, half, rest] = q[k, to, rest].astype(BF)
-            thirds[n]().wait_recv()
-            t[k, half, mine] = (q[k, to, mine] + r[k, half].astype(F32)).astype(BF)
-            fourths[n]().start()
+            t[k] = q[k].astype(BF)
+            for d in (2, 1, 3):
+                direct_copies(k, d, True)[n]().start()
+
+    def direct_sum(k):
+        one, two = qa[k, y], qb[k, x]
+        for d in (1, 3, 2):
+            for copy in direct_copies(k, d, False):
+                copy().wait_recv()
+            one = one + rda[k, lax.rem(y + d, NY)].astype(F32)
+            two = two + rdb[k, lax.rem(x + d, NX)].astype(F32)
+        return one, two
 
     def stage_last(k):
-        for copy in fourth_copies(k):
-            copy().wait_recv()
-        real = qa[k, y] + ra4[k, 0].astype(F32) + ra4[k, 1].astype(F32)
-        imag = qb[k, x] + rb4[k, 0].astype(F32) + rb4[k, 1].astype(F32)
-        last32[0:A] = real
-        last32[A:] = imag
-
-        @pl.when(k < NZ - 1)
-        def _():
-            sm[k, 0:A] = real.astype(BF)
-            sm[k, A:] = imag.astype(BF)
-            z_copy(k).start()
+        one, two = direct_sum(k)
+        sm[k, 0:AR] = one.astype(BF)
+        sm[k, AR:] = two.astype(BF)
+        z_copy(k).start()
 
     stages = [
-        (stage_merge, 0),
-        (stage_patterns, 1),
-        (stage_second, 2),
-        (stage_third, 4),
-        (stage_fourth, 6),
-        (stage_last, 8),
+        (stage_merge, LAGS[0], NZ),
+        (stage_patterns, LAGS[1], NZ),
+        (stage_second, LAGS[2], NZ),
+        (stage_third, LAGS[3], NZ),
+        (stage_last, LAGS[4], NZ - 1),
     ]
 
     def flow(t, carry):
-        for stage, lag in stages:
-
-            @pl.when(jnp.logical_and(t >= lag, t < NZ + lag))
+        for stage, lag, count in stages:
+
+            @pl.when(jnp.logical_and(t >= lag, t < count + lag))
             def _(stage=stage, lag=lag):
                 with jax.named_scope(stage.__name__):
                     stage(t - lag)
 
         return carry
 
-    lax.fori_loop(0, NZ + stages[-1][1], flow, 0)
-
-    total = last32[...]
+    lax.fori_loop(0, NZ - 1 + stages[-1][1], flow, 0)
+
+    with jax.named_scope("d_wait"):
+        one, two = direct_sum(NZ - 1)
+        total = jnp.concatenate([one, two], axis=0)
     with jax.named_scope("z_wait"):
         for k in range(NZ - 1):
             z_copy(k).wait_recv()
@@ -390,57 +369,59 @@
     inten[...] = intensity
     mx[...] = jnp.max(intensity, axis=0, keepdims=True)
 
-    slot = x * NC + c
-    m1[slot] = mx[...]
-
-    def near(i, sender):
-        other = lax.rem(slot + i, NX * NC)
-        at = slot if sender else other
-        to = dev(other // NC, y, z, lax.rem(other, NC))
-        return remote(mx, m1.at[at], ms.at[i], mr.at[at], to)()
-
-    for i in range(1, NX * NC):
-        near(i, True).start()
+    near = remote(mx, m1.at[1], ms.at[0], mr.at[CHIPS], to_sib)()
+    near.start()
     with jax.named_scope("near_wait"):
-        for i in range(1, NX * NC):
-            near(i, False).wait_recv()
-    mz[...] = jnp.max(m1[...], axis=0)
-    m2[z] = mz[...]
+        near.wait_recv()
+    mz[...] = jnp.maximum(mx[...], m1[1])
+    m2[chip] = mz[...]
 
     def far(i, sender):
-        oz = lax.rem(z + i, NZ)
-        at = z if sender else oz
-        return remote(mz, m2.at[at], ms.at[NZ + i], mr.at[NZ + at], dev(x, y, oz, c))()
-
-    for i in range(1, NZ):
+        other = lax.rem(chip + i, CHIPS)
+        at = chip if sender else other
+        return remote(mz, m2.at[at], ms.at[i], mr.at[at], (other * NC + c, y))()
+
+    def far_send(i, carry):
         far(i, True).start()
-    with jax.named_scope("far_wait"):
-        for i in range(1, NZ):
-            far(i, False).wait_recv()
-    top_out[...] = jnp.max(m2[...], axis=0)
-
-    def drain_f(i, carry):
-        f_copy(i).wait_send()
         return carry
 
+    def far_wait(i, carry):
+        far(i, False).wait_recv()
+        return carry
+
+    with jax.named_scope("far_send"):
+        lax.fori_loop(1, CHIPS, far_send, 0)
     def drain(k, carry):
         pair_copy(k).wait_send()
-        for copies in (first_copies(k), second_copies(k), third_copies(k), fourth_copies(k)):
+        for copies in (first_copies(k), second_copies(k)):
             for copy in copies:
+                copy().wait_send()
+
+        for d in range(1, NX):
+            for copy in direct_copies(k, d, True):
                 copy().wait_send()
 
         @pl.when(k < NZ - 1)
         def _():
             z_copy(k).wait_send()
-            near(k + 1, True).wait_send()
-            far(k + 1, True).wait_send()
 
         return carry
 
+    def drain_far(i, carry):
+        far(i, True).wait_send()
+        return carry
+
     with jax.named_scope("drain"):
-        lax.fori_loop(0, CHIPS - NX, drain_f, 0)
-        lax.fori_loop(CHIPS - NX + 1, CHIPS, drain_f, 0)
+        for i in range(CHIPS):
+            if i != CHIPS - NX:
+                f_copy(i).wait_send()
         lax.fori_loop(0, NZ, drain, 0)
+        near.wait_send()
+
+    with jax.named_scope("far_wait"):
+        lax.fori_loop(1, CHIPS, far_wait, 0)
+    top_out[...] = jnp.max(m2[...], axis=0)
+    lax.fori_loop(1, CHIPS, drain_far, 0)
 
 
 def finish(inten, top, out, peak):
@@ -484,33 +465,28 @@
             vm((2 * LR, 2 * NE), BF),
             vm((NZ, NX, 3, R, 2 * NE), BF),
             vm((CHIPS, NC * R, 2 * A), BF),
-            vm((NZ, NX, NY, A, EQ), F32),
-            vm((NZ, NY, NX, A, EQ), F32),
-            vm((NZ, 4, A, EQ), BF),
-            vm((NZ, 4, A, EQ), BF),
-            vm((NZ, 2, 4, A, EQ), BF),
-            vm((NZ, 2, 4, A, EQ), BF),
-            vm((NZ, 2, 2, A, EQ), BF),
-            vm((NZ, 2, 2, A, EQ), BF),
-            vm((NZ, 2, 4, A, EQ), BF),
-            vm((NZ, 2, 4, A, EQ), BF),
-            vm((NZ, NY, A, EQ), F32),
-            vm((NZ, NX, A, EQ), F32),
-            vm((NZ, A, EQ), BF),
-            vm((NZ, A, EQ), BF),
-            vm((NZ, 2, A, EQ), BF),
-            vm((NZ, 2, A, EQ), BF),
-            vm((NZ, 2, A // 2, EQ), BF),
-            vm((NZ, 2, A // 2, EQ), BF),
-            vm((NZ, 2, A, EQ), BF),
-            vm((NZ, 2, A, EQ), BF),
+            vm((NZ, NX, NY, AR, EQ), F32),
+            vm((NZ, NY, NX, BR, EQ), F32),
+            vm((NZ, 4, AR, EQ), BF),
+            vm((NZ, 4, BR, EQ), BF),
+            vm((NZ, 2, 4, AR, EQ), BF),
+            vm((NZ, 2, 4, BR, EQ), BF),
+            vm((NZ, 2, 2, AR, EQ), BF),
+            vm((NZ, 2, 2, BR, EQ), BF),
+            vm((NZ, 2, 4, AR, EQ), BF),
+            vm((NZ, 2, 4, BR, EQ), BF),
+            vm((NZ, NY, AR, EQ), F32),
+            vm((NZ, NX, BR, EQ), F32),
             vm((NZ, 2 * A, EQ), BF),
             vm((NZ, 2 * A, EQ), BF),
-            vm((2 * A, EQ), F32),
+            vm((NZ, NY, AR, EQ), BF),
+            vm((NZ, NX, BR, EQ), BF),
+            vm((NZ, NY, AR, EQ), BF),
+            vm((NZ, NX, BR, EQ), BF),
             vm((1, EQ), F32),
-            vm((NX * NC, 1, EQ), F32),
+            vm((2, 1, EQ), F32),
             vm((1, EQ), F32),
-            vm((NZ, 1, EQ), F32),
+            vm((CHIPS, 1, EQ), F32),
             dma((4,)),
             dma((CHIPS,)),
             dma((CHIPS,)),
@@ -518,12 +494,12 @@
             dma((NZ,)),
             dma((NZ, 8)),
             dma((NZ, 8)),
-            dma((NZ, 8)),
-            dma((NZ, 8)),
             dma((NZ,)),
             dma((NZ,)),
-            dma((2 * NZ,)),
-            dma((2 * NZ,)),
+            dma((NZ, NX + NY)),
+            dma((NZ, NX + NY)),
+            dma((CHIPS,)),
+            dma((CHIPS + 1,)),
         ],
         compiler_params=pltpu.CompilerParams(
             collective_id=0, has_side_effects=True, vmem_limit_bytes=62 * 1024 * 1024

time: 72.6 us -> 68.6 us (0.945)
  Pallas kernels: 69.3 us -> 65.3 us
    pallas_call x1, Pallas kernels: 67.9 us -> 63.9 us  [body(): pl.pallas_call(kernel, out_shape=shapes, in_specs=[pl.BlockSpec(memory_sp...]
where the time goes in v1:
time: 68.6 us; the launch traced here: 68.3 us
  Pallas kernels  65.3 us (95%)
  local copies, waits for them, and re-layouts  2.45 us (4%)
    pallas_call x1, Pallas kernels, body(): pl.pallas_call(kernel, out_shape=shapes, in_specs=[pl.BlockSpec(memory_sp...  63.9 us
    dynamic_slice x1, local copies, waits for them, and re-layouts, body(): lax.dynamic_index_in_dim(angle_factor, lax.axis_index('grp'), 1, keepdims...  1.54 us
    pallas_call x1, Pallas kernels, body(): pl.pallas_call(finish, out_shape=shapes, in_specs=[invm, invm], out_specs...  1.39 us

profile of v1, /device:TPU:1, one launch (start us, length us, event | category | flops | bytes accessed | tf_op | source)
XLA Modules:
  0.0 68.3 jit_solution(157241248444116442)
XLA Ops:
  0.6 1.5 %constant_dynamic-slice_fusion = bf16[64,1,2,2560]{3,2,1,0:T(2,128)(2,1)S(1)} fusion(bf16[64,4,2,2560]{3,2,1,0:T(2,128)(2,1)} %param.11, s32[]{:T(128)S(6)} %select_n.4), kind=kLoop, calls=%fused_computation | loop fusion | bytes 1310724 | tf_op jit(solution)/shard_map/jit(dynamic_index_in_dim)/dynamic_slice | solution.py:433
  2.2 0.9 %copy.9 = bf16[64,1,2,2560]{3,0,2,1:T(8,128)(2,1)} copy(bf16[64,1,2,2560]{3,2,1,0:T(2,128)(2,1)S(1)} %constant_dynamic-slice_fusion) | data formatting | bytes 1310720
  3.1 63.9 %shard_map.77 = (f32[64,128]{1,0:T(8,128)}, f32[1,128]{1,0:T(1,128)}) custom-call(s32[8]{0:T(128)} %cnt.1, s32[1,2048]{1,0:T(1,128)} %bitcast.12, bf16[2048,1024]{1,0:T(8,128)(2,1)} %x_hbm.1, bf16[2,40,2048]{2,1,0:T(8,128)(2,1)} %basis_hbm.1, bf16[640,2560]{1,0:T(8,128)(2,1)} %bitcast.10, bf16[128,2560]{1,0:T(8,128)(2,1)} %bitcast.11), custom_call_target="tpu_custom_call" | custom-call | tf_op jit(solution)/shard_map/pallas_call | solution.py:445
  67.0 1.4 %shard_map.78 = (f32[64,128]{1,0:T(8,128)}, f32[1,128]{1,0:T(1,128)}) custom-call(f32[64,128]{1,0:T(8,128)} %get-tuple-element.6.inten, f32[1,128]{1,0:T(1,128)} %get-tuple-element.7.top), custom_call_target="tpu_custom_call" | custom-call | tf_op jit(solution)/shard_map/pallas_call | solution.py:515

commit v2 on v1

--- a/solution.py
+++ b/solution.py
@@ -21,8 +21,8 @@
 EQ = NE // NY
 LR = LEAF * R
 GX = NZ * NC * R
-OFFSETS = (1, 7, 2, 6, 4, 3, 5, 0)
-LAGS = (0, 1, 3, 6, 8)
+OFFSETS = (1, 7, 2, 5, 3, 4, 6, 0)
+LAGS = (0, 1, 3, 6, 9)
 AR = 64
 BR = 2 * A - AR
 
@@ -36,14 +36,17 @@
 
 
 def kernel(
-    cnt,
-    box,
+    cnt_hbm,
+    box_hbm,
     x_hbm,
     basis_hbm,
     mt_hbm,
     own_hbm,
+    inten_hbm,
+    top_out,
+    cnt,
+    box,
     inten,
-    top_out,
     xv,
     basis,
     mt,
@@ -127,7 +130,14 @@
     loads = [
         pltpu.make_async_copy(a, b, ld_sem.at[i])
         for i, (a, b) in enumerate(
-            [(own_hbm, own), (basis_hbm, basis), (x_hbm, xv), (mt_hbm, mt)]
+            [
+                (own_hbm.at[:, y], own),
+                (cnt_hbm, cnt),
+                (box_hbm, box),
+                (basis_hbm, basis),
+                (x_hbm, xv),
+                (mt_hbm, mt),
+            ]
         )
     ]
     for copy in loads:
@@ -147,8 +157,19 @@
     for to in greeted:
         pl.semaphore_signal(barrier, inc=1, device_id=to, device_id_type=MESH)
 
+    with jax.named_scope("turn_f"):
+        loads[0].wait()
+
+        for i in range(NX * GX // 128):
+            span = slice(i * 128, (i + 1) * 128)
+            pair = own[:, :, span]
+            both = jnp.concatenate([pair[:, 0, :], pair[:, 1, :]], axis=0)
+            ft[span, :] = jnp.transpose(both)
+        rf[chip] = ft3[chip]
+
     with jax.named_scope("build"):
-        loads[1].wait()
+        for copy in loads[1:4]:
+            copy.wait()
         scale = [
             lax.rsqrt(jnp.full((8, 128), cnt[b], jnp.int32).astype(F32))[0:1, 0:1]
             for b in range(LEAF)
@@ -170,14 +191,6 @@
 
         lax.fori_loop(0, S_DEV // width, build, 0)
 
-    with jax.named_scope("turn_f"):
-        loads[0].wait()
-
-        for i in range(NX * GX // 128):
-            span = slice(i * 128, (i + 1) * 128)
-            ft[span, :] = jnp.transpose(own[:, span])
-        rf[chip] = ft3[chip]
-
     with jax.named_scope("barrier"):
         pl.semaphore_wait(barrier, CHIPS - 1 + len(greeted))
 
@@ -195,8 +208,8 @@
 
     tile = 256
     with jax.named_scope("leaf"):
-        loads[2].wait()
-        loads[3].wait()
+        loads[4].wait()
+        loads[5].wait()
         turns = NX * GX // 128 // (NE // tile)
 
         def leaf(i, carry):
@@ -340,9 +353,9 @@
 
     stages = [
         (stage_merge, LAGS[0], NZ),
-        (stage_patterns, LAGS[1], NZ),
         (stage_second, LAGS[2], NZ),
         (stage_third, LAGS[3], NZ),
+        (stage_patterns, LAGS[1], NZ),
         (stage_last, LAGS[4], NZ - 1),
     ]
 
@@ -367,6 +380,8 @@
             total = total + rz[k].astype(F32)
     intensity = total[:A] * total[:A] + total[A:] * total[A:]
     inten[...] = intensity
+    save = pltpu.make_async_copy(inten, inten_hbm, ld_sem.at[6])
+    save.start()
     mx[...] = jnp.max(intensity, axis=0, keepdims=True)
 
     near = remote(mx, m1.at[1], ms.at[0], mr.at[CHIPS], to_sib)()
@@ -422,6 +437,7 @@
         lax.fori_loop(1, CHIPS, far_wait, 0)
     top_out[...] = jnp.max(m2[...], axis=0)
     lax.fori_loop(1, CHIPS, drain_far, 0)
+    save.wait()
 
 
 def finish(inten, top, out, peak):
@@ -430,8 +446,6 @@
 
 
 def body(currents, leaf_basis, leaf_box, box_count, merge_factor, angle_factor):
-    own = lax.dynamic_index_in_dim(angle_factor, lax.axis_index("grp"), 1, keepdims=False)
-    own = jnp.transpose(own, (1, 0, 2)).reshape(2 * A, NX * GX)
     turned = jnp.transpose(merge_factor, (0, 2, 1)).reshape(2 * LR, NX * GX)
 
     vm = pltpu.VMEM
@@ -445,20 +459,16 @@
     inten, top = pl.pallas_call(
         kernel,
         out_shape=shapes,
-        in_specs=[
-            pl.BlockSpec(memory_space=pltpu.SMEM),
-            invm,
-            anyspace,
-            anyspace,
-            anyspace,
-            anyspace,
-        ],
-        out_specs=(invm, invm),
+        in_specs=[anyspace] * 6,
+        out_specs=(anyspace, invm),
         scratch_shapes=[
+            pltpu.SMEM((LEAF,), jnp.int32),
+            vm((1, S_DEV), jnp.int32),
+            vm((A, EQ), F32),
             vm((S_DEV, 2 * NE), BF),
             vm((2, R, S_DEV), BF),
             vm((2 * LR, NX * GX), BF),
-            vm((2 * A, NX * GX), BF),
+            vm((A, 2, NX * GX), BF),
             vm((NX * GX, 2 * A), BF),
             vm((2 * LR, S_DEV), BF),
             vm((NX * GX, 2 * LR), BF),
@@ -487,7 +497,7 @@
             vm((2, 1, EQ), F32),
             vm((1, EQ), F32),
             vm((CHIPS, 1, EQ), F32),
-            dma((4,)),
+            dma((7,)),
             dma((CHIPS,)),
             dma((CHIPS,)),
             dma((NZ,)),
@@ -510,7 +520,7 @@
         currents,
         leaf_basis,
         turned,
-        own,
+        angle_factor,
     )
     normalized, peak = pl.pallas_call(
         finish,

time: 68.6 us -> 65.8 us (0.959)
  local copies, waits for them, and re-layouts: 2.45 us -> 0 us
    dynamic_slice x1 -> x0, local copies, waits for them, and re-layouts: 1.54 us -> none  [body(): lax.dynamic_index_in_dim(angle_factor, lax.axis_index('grp'), 1, keepdims...]
    unnamed x1 -> x0, local copies, waits for them, and re-layouts: 0.91 us -> none
where the time goes in v2:
time: 65.8 us; the launch traced here: 65.6 us
  Pallas kernels  65 us (99%)
    pallas_call x1, Pallas kernels, body(): pl.pallas_call(kernel, out_shape=shapes, in_specs=[anyspace] * 6, out_spe...  63.6 us
    pallas_call x1, Pallas kernels, body(): pl.pallas_call(finish, out_shape=shapes, in_specs=[invm, invm], out_specs...  1.39 us

profile of v2, /device:TPU:1, one launch (start us, length us, event | category | flops | bytes accessed | tf_op | source)
XLA Modules:
  0.0 65.6 jit_solution(14592023422081630654)
XLA Ops:
  0.6 63.6 %shard_map.77 = (f32[64,128]{1,0:T(8,128)}, f32[1,128]{1,0:T(1,128)}) custom-call(s32[8]{0:T(128)} %cnt_hbm.1, s32[1,2048]{1,0:T(1,128)} %bitcast.6, bf16[2048,1024]{1,0:T(8,128)(2,1)} %x_hbm.1, bf16[2,40,2048]{2,1,0:T(8,128)(2,1)} %basis_hbm.1, bf16[640,2560]{1,0:T(8,128)(2,1)} %bitcast.5, bf16[64,4,2,2560]{3,2,1,0:T(2,128)(2,1)} %own_hbm.1), custom_call_target="tpu_custom_call" | custom-call | tf_op jit(solution)/shard_map/pallas_call | solution.py:459
  64.2 1.4 %shard_map.78 = (f32[64,128]{1,0:T(8,128)}, f32[1,128]{1,0:T(1,128)}) custom-call(f32[64,128]{1,0:T(8,128)} %get-tuple-element.6.inten, f32[1,128]{1,0:T(1,128)} %get-tuple-element.7.top), custom_call_target="tpu_custom_call" | custom-call | tf_op jit(solution)/shard_map/pallas_call | solution.py:525

commit v3 on v2

--- a/solution.py
+++ b/solution.py
@@ -22,9 +22,10 @@
 LR = LEAF * R
 GX = NZ * NC * R
 OFFSETS = (1, 7, 2, 5, 3, 4, 6, 0)
-LAGS = (0, 1, 3, 6, 9)
+LAGS = (0, 1, 4, 7, 10)
 AR = 64
 BR = 2 * A - AR
+RAW = 4
 
 
 def tdot(a, b):
@@ -71,6 +72,10 @@
     qb,
     sm,
     rz,
+    wa,
+    wb,
+    va,
+    vb,
     tda,
     tdb,
     rda,
@@ -90,6 +95,8 @@
     zr,
     ds,
     dr,
+    ws,
+    wr,
     ms,
     mr,
 ):
@@ -269,6 +276,13 @@
             ),
         ]
 
+    def raw_copies():
+        up, down = lax.rem(z + 1, NZ), lax.rem(z + NZ - 1, NZ)
+        return [
+            remote(wa, va, ws.at[0], wr.at[0], dev(x, y, up, c)),
+            remote(wb, vb, ws.at[1], wr.at[1], dev(x, y, down, c)),
+        ]
+
     def z_copy(k):
         return remote(sm.at[k], rz.at[k], zs.at[k], zr.at[k], dev(x, y, target_z(k), c))()
 
@@ -305,10 +319,36 @@
                 if AR < A:
                     pb[k, j, i, 0 : A - AR] = real[AR:, j * EQ : (j + 1) * EQ]
                 pb[k, j, i, A - AR :] = imag[:, j * EQ : (j + 1) * EQ]
-        ta1[k] = pa[k, xo].astype(BF)
-        tb1[k] = pb[k, yo].astype(BF)
-        for copy in first_copies(k):
-            copy().start()
+
+        @pl.when(k == 0)
+        def _():
+            wa[...] = pa[0].astype(BF)
+
+        @pl.when(k == 1)
+        def _():
+            wb[...] = pb[1].astype(BF)
+
+        @pl.when(k == NZ - 1)
+        def _():
+            with jax.named_scope("raw_wait"):
+                for copy in raw_copies():
+                    copy().wait_recv()
+            pa[NZ - 1] = pa[NZ - 1] + va[...].astype(F32)
+            pb[NZ - 1] = pb[NZ - 1] + vb[...].astype(F32)
+
+        firsts = first_copies(k)
+        for n, (p, t, far_side) in enumerate([(pa, ta1, xo), (pb, tb1, yo)]):
+
+            @pl.when(k != n)
+            def _(n=n, p=p, t=t, far_side=far_side):
+                t[k] = p[k, far_side].astype(BF)
+                firsts[n]().start()
+                firsts[n + 2]().start()
+
+        @pl.when(k == RAW)
+        def _():
+            for copy in raw_copies():
+                copy().start()
 
     def stage_second(k):
         firsts, seconds = first_copies(k), second_copies(k)
@@ -321,34 +361,46 @@
             ]
         ):
             mine, rest = (slice(0, 2), slice(2, 4)) if half == 0 else (slice(2, 4), slice(0, 2))
-            t[k, half, rest] = p[k, to, rest].astype(BF)
-            firsts[n]().wait_recv()
-            t[k, half, mine] = (p[k, to, mine] + r[k, half].astype(F32)).astype(BF)
-            seconds[n]().start()
+
+            @pl.when(k != n % 2)
+            def _(n=n, p=p, t=t, r=r, to=to, half=half, mine=mine, rest=rest):
+                t[k, half, rest] = p[k, to, rest].astype(BF)
+                firsts[n]().wait_recv()
+                t[k, half, mine] = (p[k, to, mine] + r[k, half].astype(F32)).astype(BF)
+                seconds[n]().start()
 
     def stage_third(k):
         seconds = second_copies(k)
         for n, (p, q, t, r, me) in enumerate([(pa, qa, tda, ra2, x), (pb, qb, tdb, rb2, y)]):
-            seconds[n]().wait_recv()
-            seconds[n + 2]().wait_recv()
-            q[k] = p[k, me] + r[k, 0].astype(F32) + r[k, 1].astype(F32)
-            t[k] = q[k].astype(BF)
-            for d in (2, 1, 3):
-                direct_copies(k, d, True)[n]().start()
-
-    def direct_sum(k):
-        one, two = qa[k, y], qb[k, x]
+
+            @pl.when(k != n)
+            def _(n=n, p=p, q=q, t=t, r=r, me=me):
+                seconds[n]().wait_recv()
+                seconds[n + 2]().wait_recv()
+                q[k] = p[k, me] + r[k, 0].astype(F32) + r[k, 1].astype(F32)
+                t[k] = q[k].astype(BF)
+                for d in (2, 1, 3):
+                    direct_copies(k, d, True)[n]().start()
+
+    def direct_sum(k, n):
+        q, r, me, size = ((qa, rda, y, NY), (qb, rdb, x, NX))[n]
+        total = q[k, me]
         for d in (1, 3, 2):
-            for copy in direct_copies(k, d, False):
-                copy().wait_recv()
-            one = one + rda[k, lax.rem(y + d, NY)].astype(F32)
-            two = two + rdb[k, lax.rem(x + d, NX)].astype(F32)
-        return one, two
+            direct_copies(k, d, False)[n]().wait_recv()
+            total = total + r[k, lax.rem(me + d, size)].astype(F32)
+        return total
 
     def stage_last(k):
-        one, two = direct_sum(k)
-        sm[k, 0:AR] = one.astype(BF)
-        sm[k, AR:] = two.astype(BF)
+        for n, rows in enumerate((slice(0, AR), slice(AR, 2 * A))):
+
+            @pl.when(k != n)
+            def _(n=n, rows=rows):
+                sm[k, rows] = direct_sum(k, n).astype(BF)
+
+            @pl.when(k == n)
+            def _(rows=rows):
+                sm[k, rows] = jnp.zeros((rows.stop - rows.start, EQ), BF)
+
         z_copy(k).start()
 
     stages = [
@@ -372,8 +424,7 @@
     lax.fori_loop(0, NZ - 1 + stages[-1][1], flow, 0)
 
     with jax.named_scope("d_wait"):
-        one, two = direct_sum(NZ - 1)
-        total = jnp.concatenate([one, two], axis=0)
+        total = jnp.concatenate([direct_sum(NZ - 1, n) for n in range(2)], axis=0)
     with jax.named_scope("z_wait"):
         for k in range(NZ - 1):
             z_copy(k).wait_recv()
@@ -396,25 +447,24 @@
         at = chip if sender else other
         return remote(mz, m2.at[at], ms.at[i], mr.at[at], (other * NC + c, y))()
 
-    def far_send(i, carry):
-        far(i, True).start()
-        return carry
-
     def far_wait(i, carry):
         far(i, False).wait_recv()
         return carry
 
     with jax.named_scope("far_send"):
-        lax.fori_loop(1, CHIPS, far_send, 0)
+        for i in range(CHIPS // 2, CHIPS // 2 + CHIPS - 1):
+            far(1 + i % (CHIPS - 1), True).start()
     def drain(k, carry):
         pair_copy(k).wait_send()
-        for copies in (first_copies(k), second_copies(k)):
-            for copy in copies:
-                copy().wait_send()
-
-        for d in range(1, NX):
-            for copy in direct_copies(k, d, True):
-                copy().wait_send()
+        for n in range(2):
+
+            @pl.when(k != n)
+            def _(n=n):
+                for copies in (first_copies(k), second_copies(k)):
+                    copies[n]().wait_send()
+                    copies[n + 2]().wait_send()
+                for d in range(1, NX):
+                    direct_copies(k, d, True)[n]().wait_send()
 
         @pl.when(k < NZ - 1)
         def _():
@@ -432,6 +482,8 @@
                 f_copy(i).wait_send()
         lax.fori_loop(0, NZ, drain, 0)
         near.wait_send()
+        for copy in raw_copies():
+            copy().wait_send()
 
     with jax.named_scope("far_wait"):
         lax.fori_loop(1, CHIPS, far_wait, 0)
@@ -489,6 +541,10 @@
             vm((NZ, NX, BR, EQ), F32),
             vm((NZ, 2 * A, EQ), BF),
             vm((NZ, 2 * A, EQ), BF),
+            vm((NX, NY, AR, EQ), BF),
+            vm((NY, NX, BR, EQ), BF),
+            vm((NX, NY, AR, EQ), BF),
+            vm((NY, NX, BR, EQ), BF),
             vm((NZ, NY, AR, EQ), BF),
             vm((NZ, NX, BR, EQ), BF),
             vm((NZ, NY, AR, EQ), BF),
@@ -508,6 +564,8 @@
             dma((NZ,)),
             dma((NZ, NX + NY)),
             dma((NZ, NX + NY)),
+            dma((2,)),
+            dma((2,)),
             dma((CHIPS,)),
             dma((CHIPS + 1,)),
         ],

time: 65.8 us -> 63.5 us (0.965)
  Pallas kernels: 65 us -> 62.7 us
    pallas_call x1, Pallas kernels: 63.6 us -> 61.3 us  [body(): pl.pallas_call(kernel, out_shape=shapes, in_specs=[anyspace] * 6, out_spe...]
where the time goes in v3:
time: 63.5 us; the launch traced here: 63.4 us
  Pallas kernels  62.7 us (99%)
  between operations  0.64 us (1%)
    pallas_call x1, Pallas kernels, body(): pl.pallas_call(kernel, out_shape=shapes, in_specs=[anyspace] * 6, out_spe...  61.3 us
    pallas_call x1, Pallas kernels, body(): pl.pallas_call(finish, out_shape=shapes, in_specs=[invm, invm], out_specs...  1.39 us

profile of v3, /device:TPU:1, one launch (start us, length us, event | category | flops | bytes accessed | tf_op | source)
XLA Modules:
  0.0 63.4 jit_solution(5813204581382750093)
XLA Ops:
  0.6 61.3 %shard_map.77 = (f32[64,128]{1,0:T(8,128)}, f32[1,128]{1,0:T(1,128)}) custom-call(s32[8]{0:T(128)} %cnt_hbm.1, s32[1,2048]{1,0:T(1,128)} %bitcast.6, bf16[2048,1024]{1,0:T(8,128)(2,1)} %x_hbm.1, bf16[2,40,2048]{2,1,0:T(8,128)(2,1)} %basis_hbm.1, bf16[640,2560]{1,0:T(8,128)(2,1)} %bitcast.5, bf16[64,4,2,2560]{3,2,1,0:T(2,128)(2,1)} %own_hbm.1), custom_call_target="tpu_custom_call" | custom-call | tf_op jit(solution)/shard_map/pallas_call | solution.py:511
  62.0 1.4 %shard_map.78 = (f32[64,128]{1,0:T(8,128)}, f32[1,128]{1,0:T(1,128)}) custom-call(f32[64,128]{1,0:T(8,128)} %get-tuple-element.6.inten, f32[1,128]{1,0:T(1,128)} %get-tuple-element.7.top), custom_call_target="tpu_custom_call" | custom-call | tf_op jit(solution)/shard_map/pallas_call | solution.py:583

commit v4 on v3

--- a/solution.py
+++ b/solution.py
@@ -205,7 +205,7 @@
         k, dx = i // NX, i % NX
         tx, tz = lax.rem(x + dx, NX), lax.rem(z + NZ - OFFSETS[k], NZ)
         return remote(
-            ft3.at[tx * NZ + tz], rf.at[chip], fs_sem.at[i], fr_sem.at[chip], dev(tx, y, tz, c)
+            ft3.at[tx * NZ + tz], rf.at[chip], fs_sem.at[0], fr_sem.at[z], dev(tx, y, tz, c)
         )()
 
     with jax.named_scope("f_send"):
@@ -237,23 +237,26 @@
 
         lax.fori_loop(0, NE // tile, leaf, 0)
 
+    def bulk(ref, send, recv):
+        return remote(ref, ref, send, recv, to_sib)()
+
     def pair_copy(k):
-        return remote(bb.at[k, :, 2], bb.at[k, :, c], ps_sem.at[k], pr_sem.at[k], to_sib)()
+        return remote(bb.at[k, :, 2], bb.at[k, :, c], ps_sem.at[0], pr_sem.at[k], to_sib)()
 
     def first_copies(k):
         return [
-            remote(ta1.at[k, 0:2], ra1.at[k, 0], s1.at[k, 0], r1.at[k, 0], to_xp),
-            remote(tb1.at[k, 0:2], rb1.at[k, 0], s1.at[k, 1], r1.at[k, 1], to_yp),
-            remote(ta1.at[k, 2:4], ra1.at[k, 1], s1.at[k, 2], r1.at[k, 2], to_xm),
-            remote(tb1.at[k, 2:4], rb1.at[k, 1], s1.at[k, 3], r1.at[k, 3], to_ym),
+            remote(ta1.at[k, 0:2], ra1.at[k, 0], s1.at[0], r1.at[k, 0], to_xp),
+            remote(tb1.at[k, 0:2], rb1.at[k, 0], s1.at[1], r1.at[k, 1], to_yp),
+            remote(ta1.at[k, 2:4], ra1.at[k, 1], s1.at[0], r1.at[k, 2], to_xm),
+            remote(tb1.at[k, 2:4], rb1.at[k, 1], s1.at[1], r1.at[k, 3], to_ym),
         ]
 
     def second_copies(k):
         return [
-            remote(ta2.at[k, 0], ra2.at[k, 0], s1.at[k, 4], r1.at[k, 4], to_xp),
-            remote(tb2.at[k, 0], rb2.at[k, 0], s1.at[k, 5], r1.at[k, 5], to_yp),
-            remote(ta2.at[k, 1], ra2.at[k, 1], s1.at[k, 6], r1.at[k, 6], to_xm),
-            remote(tb2.at[k, 1], rb2.at[k, 1], s1.at[k, 7], r1.at[k, 7], to_ym),
+            remote(ta2.at[k, 0], ra2.at[k, 0], s1.at[2], r1.at[k, 4], to_xp),
+            remote(tb2.at[k, 0], rb2.at[k, 0], s1.at[3], r1.at[k, 5], to_yp),
+            remote(ta2.at[k, 1], ra2.at[k, 1], s1.at[2], r1.at[k, 4], to_xm),
+            remote(tb2.at[k, 1], rb2.at[k, 1], s1.at[3], r1.at[k, 5], to_ym),
         ]
 
     def direct_copies(k, d, sender):
@@ -263,15 +266,15 @@
             remote(
                 tda.at[k, oy],
                 rda.at[k, ty],
-                ds.at[k, d],
-                dr.at[k, ty],
+                ds.at[0],
+                dr.at[k, 0],
                 dev(x, oy, z, c),
             ),
             remote(
                 tdb.at[k, ox],
                 rdb.at[k, tx],
-                ds.at[k, NY + d],
-                dr.at[k, NY + tx],
+                ds.at[1],
+                dr.at[k, 1],
                 dev(ox, y, z, c),
             ),
         ]
@@ -284,7 +287,7 @@
         ]
 
     def z_copy(k):
-        return remote(sm.at[k], rz.at[k], zs.at[k], zr.at[k], dev(x, y, target_z(k), c))()
+        return remote(sm.at[k], rz.at[k], zs.at[0], zr.at[0], dev(x, y, target_z(k), c))()
 
     def stage_merge(k):
         left = mm4[:, target_z(k)].reshape(NX * NC * R, 2 * LR)
@@ -299,16 +302,14 @@
     def stage_patterns(k):
         tz = target_z(k)
 
-        def arrived(i, carry):
-            at = i * NZ + tz
-
-            @pl.when(at != chip)
-            def _():
-                remote(ft3.at[0], rf.at[at], fs_sem.at[0], fr_sem.at[at], to_sib)().wait_recv()
-
-            return carry
-
-        lax.fori_loop(0, NX, arrived, 0)
+        @pl.when(k < NZ - 1)
+        def _():
+            bulk(rf.at[pl.ds(0, NX)], fs_sem.at[0], fr_sem.at[tz]).wait_recv()
+
+        @pl.when(k == NZ - 1)
+        def _():
+            bulk(rf.at[pl.ds(0, NX - 1)], fs_sem.at[0], fr_sem.at[tz]).wait_recv()
+
         pair_copy(k).wait_recv()
         for i in range(NX):
             q = tdot(rf[i * NZ + tz], bb[k, i, 0:2].reshape(NC * R, 2 * NE))
@@ -370,13 +371,11 @@
                 seconds[n]().start()
 
     def stage_third(k):
-        seconds = second_copies(k)
         for n, (p, q, t, r, me) in enumerate([(pa, qa, tda, ra2, x), (pb, qb, tdb, rb2, y)]):
 
             @pl.when(k != n)
             def _(n=n, p=p, q=q, t=t, r=r, me=me):
-                seconds[n]().wait_recv()
-                seconds[n + 2]().wait_recv()
+                bulk(r.at[k], s1.at[2 + n], r1.at[k, 4 + n]).wait_recv()
                 q[k] = p[k, me] + r[k, 0].astype(F32) + r[k, 1].astype(F32)
                 t[k] = q[k].astype(BF)
                 for d in (2, 1, 3):
@@ -385,8 +384,8 @@
     def direct_sum(k, n):
         q, r, me, size = ((qa, rda, y, NY), (qb, rdb, x, NX))[n]
         total = q[k, me]
+        bulk(r.at[k, pl.ds(0, NX - 1)], ds.at[n], dr.at[k, n]).wait_recv()
         for d in (1, 3, 2):
-            direct_copies(k, d, False)[n]().wait_recv()
             total = total + r[k, lax.rem(me + d, size)].astype(F32)
         return total
 
@@ -426,8 +425,8 @@
     with jax.named_scope("d_wait"):
         total = jnp.concatenate([direct_sum(NZ - 1, n) for n in range(2)], axis=0)
     with jax.named_scope("z_wait"):
+        bulk(rz.at[pl.ds(0, NZ - 1)], zs.at[0], zr.at[0]).wait_recv()
         for k in range(NZ - 1):
-            z_copy(k).wait_recv()
             total = total + rz[k].astype(F32)
     intensity = total[:A] * total[:A] + total[A:] * total[A:]
     inten[...] = intensity
@@ -435,60 +434,38 @@
     save.start()
     mx[...] = jnp.max(intensity, axis=0, keepdims=True)
 
-    near = remote(mx, m1.at[1], ms.at[0], mr.at[CHIPS], to_sib)()
+    near = remote(mx, m1.at[1], ms.at[0], mr.at[0], to_sib)()
     near.start()
     with jax.named_scope("near_wait"):
         near.wait_recv()
     mz[...] = jnp.maximum(mx[...], m1[1])
     m2[chip] = mz[...]
 
-    def far(i, sender):
+    def far(i):
         other = lax.rem(chip + i, CHIPS)
-        at = chip if sender else other
-        return remote(mz, m2.at[at], ms.at[i], mr.at[at], (other * NC + c, y))()
-
-    def far_wait(i, carry):
-        far(i, False).wait_recv()
-        return carry
-
+        return remote(mz, m2.at[chip], ms.at[1], mr.at[1], (other * NC + c, y))()
+
+    everyone = bulk(m2.at[pl.ds(0, CHIPS - 1)], ms.at[1], mr.at[1])
     with jax.named_scope("far_send"):
         for i in range(CHIPS // 2, CHIPS // 2 + CHIPS - 1):
-            far(1 + i % (CHIPS - 1), True).start()
-    def drain(k, carry):
-        pair_copy(k).wait_send()
-        for n in range(2):
-
-            @pl.when(k != n)
-            def _(n=n):
-                for copies in (first_copies(k), second_copies(k)):
-                    copies[n]().wait_send()
-                    copies[n + 2]().wait_send()
-                for d in range(1, NX):
-                    direct_copies(k, d, True)[n]().wait_send()
-
-        @pl.when(k < NZ - 1)
-        def _():
-            z_copy(k).wait_send()
-
-        return carry
-
-    def drain_far(i, carry):
-        far(i, True).wait_send()
-        return carry
-
+            far(1 + i % (CHIPS - 1)).start()
     with jax.named_scope("drain"):
-        for i in range(CHIPS):
-            if i != CHIPS - NX:
-                f_copy(i).wait_send()
-        lax.fori_loop(0, NZ, drain, 0)
+        bulk(ft3.at[pl.ds(0, CHIPS - 1)], fs_sem.at[0], fr_sem.at[0]).wait_send()
+        bulk(bb.at[:, :, 2], ps_sem.at[0], pr_sem.at[0]).wait_send()
+        sent = pl.ds(1, NZ - 1)
+        for n, (t1, t2, td) in enumerate([(ta1, ta2, tda), (tb1, tb2, tdb)]):
+            bulk(t1.at[sent], s1.at[n], r1.at[0, 0]).wait_send()
+            bulk(t2.at[sent], s1.at[2 + n], r1.at[0, 0]).wait_send()
+            bulk(td.at[sent, pl.ds(0, NX - 1)], ds.at[n], dr.at[0, 0]).wait_send()
+        bulk(sm.at[pl.ds(0, NZ - 1)], zs.at[0], zr.at[0]).wait_send()
         near.wait_send()
         for copy in raw_copies():
             copy().wait_send()
 
     with jax.named_scope("far_wait"):
-        lax.fori_loop(1, CHIPS, far_wait, 0)
+        everyone.wait_recv()
     top_out[...] = jnp.max(m2[...], axis=0)
-    lax.fori_loop(1, CHIPS, drain_far, 0)
+    everyone.wait_send()
     save.wait()
 
 
@@ -554,20 +531,20 @@
             vm((1, EQ), F32),
             vm((CHIPS, 1, EQ), F32),
             dma((7,)),
-            dma((CHIPS,)),
-            dma((CHIPS,)),
+            dma((1,)),
             dma((NZ,)),
+            dma((1,)),
             dma((NZ,)),
-            dma((NZ, 8)),
-            dma((NZ, 8)),
-            dma((NZ,)),
-            dma((NZ,)),
-            dma((NZ, NX + NY)),
-            dma((NZ, NX + NY)),
+            dma((4,)),
+            dma((NZ, 6)),
+            dma((1,)),
+            dma((1,)),
+            dma((2,)),
+            dma((NZ, 2)),
             dma((2,)),
             dma((2,)),
-            dma((CHIPS,)),
-            dma((CHIPS + 1,)),
+            dma((2,)),
+            dma((2,)),
         ],
         compiler_params=pltpu.CompilerParams(
             collective_id=0, has_side_effects=True, vmem_limit_bytes=62 * 1024 * 1024

time: 63.5 us -> 60.5 us (0.953)
  Pallas kernels: 62.7 us -> 59.7 us
    pallas_call x1, Pallas kernels: 61.3 us -> 58.3 us  [body(): pl.pallas_call(kernel, out_shape=shapes, in_specs=[anyspace] * 6, out_spe...]
where the time goes in v4:
time: 60.5 us; the launch traced here: 60.3 us
  Pallas kernels  59.7 us (99%)
  between operations  0.64 us (1%)
    pallas_call x1, Pallas kernels, body(): pl.pallas_call(kernel, out_shape=shapes, in_specs=[anyspace] * 6, out_spe...  58.3 us
    pallas_call x1, Pallas kernels, body(): pl.pallas_call(finish, out_shape=shapes, in_specs=[invm, invm], out_specs...  1.39 us

profile of v4, /device:TPU:1, one launch (start us, length us, event | category | flops | bytes accessed | tf_op | source)
XLA Modules:
  0.0 60.3 jit_solution(436374379492057)
XLA Ops:
  0.6 58.3 %shard_map.77 = (f32[64,128]{1,0:T(8,128)}, f32[1,128]{1,0:T(1,128)}) custom-call(s32[8]{0:T(128)} %cnt_hbm.1, s32[1,2048]{1,0:T(1,128)} %bitcast.6, bf16[2048,1024]{1,0:T(8,128)(2,1)} %x_hbm.1, bf16[2,40,2048]{2,1,0:T(8,128)(2,1)} %basis_hbm.1, bf16[640,2560]{1,0:T(8,128)(2,1)} %bitcast.5, bf16[64,4,2,2560]{3,2,1,0:T(2,128)(2,1)} %own_hbm.1), custom_call_target="tpu_custom_call" | custom-call | tf_op jit(solution)/shard_map/pallas_call | solution.py:488
  58.9 1.4 %shard_map.78 = (f32[64,128]{1,0:T(8,128)}, f32[1,128]{1,0:T(1,128)}) custom-call(f32[64,128]{1,0:T(8,128)} %get-tuple-element.6.inten, f32[1,128]{1,0:T(1,128)} %get-tuple-element.7.top), custom_call_target="tpu_custom_call" | custom-call | tf_op jit(solution)/shard_map/pallas_call | solution.py:560

commit v5 on v4

--- a/solution.py
+++ b/solution.py
@@ -152,14 +152,13 @@
 
     barrier = pltpu.get_barrier_semaphore()
 
-    def greet(i, carry):
-        other = lax.rem(chip + i, CHIPS)
+    for i in range(1, CHIPS):
         pl.semaphore_signal(
-            barrier, inc=1, device_id=(other * NC + c, y), device_id_type=MESH
+            barrier,
+            inc=1,
+            device_id=(lax.rem(chip + i, CHIPS) * NC + c, y),
+            device_id_type=MESH,
         )
-        return carry
-
-    lax.fori_loop(1, CHIPS, greet, 0)
     greeted = [to_yp, to_ym, dev(x, yo, z, c), to_sib]
     for to in greeted:
         pl.semaphore_signal(barrier, inc=1, device_id=to, device_id_type=MESH)
@@ -247,16 +246,16 @@
         return [
             remote(ta1.at[k, 0:2], ra1.at[k, 0], s1.at[0], r1.at[k, 0], to_xp),
             remote(tb1.at[k, 0:2], rb1.at[k, 0], s1.at[1], r1.at[k, 1], to_yp),
-            remote(ta1.at[k, 2:4], ra1.at[k, 1], s1.at[0], r1.at[k, 2], to_xm),
-            remote(tb1.at[k, 2:4], rb1.at[k, 1], s1.at[1], r1.at[k, 3], to_ym),
+            remote(ta1.at[k, 2:4], ra1.at[k, 1], s1.at[0], r1.at[k, 0], to_xm),
+            remote(tb1.at[k, 2:4], rb1.at[k, 1], s1.at[1], r1.at[k, 1], to_ym),
         ]
 
     def second_copies(k):
         return [
-            remote(ta2.at[k, 0], ra2.at[k, 0], s1.at[2], r1.at[k, 4], to_xp),
-            remote(tb2.at[k, 0], rb2.at[k, 0], s1.at[3], r1.at[k, 5], to_yp),
-            remote(ta2.at[k, 1], ra2.at[k, 1], s1.at[2], r1.at[k, 4], to_xm),
-            remote(tb2.at[k, 1], rb2.at[k, 1], s1.at[3], r1.at[k, 5], to_ym),
+            remote(ta2.at[k, 0], ra2.at[k, 0], s1.at[2], r1.at[k, 2], to_xp),
+            remote(tb2.at[k, 0], rb2.at[k, 0], s1.at[3], r1.at[k, 3], to_yp),
+            remote(ta2.at[k, 1], ra2.at[k, 1], s1.at[2], r1.at[k, 2], to_xm),
+            remote(tb2.at[k, 1], rb2.at[k, 1], s1.at[3], r1.at[k, 3], to_ym),
         ]
 
     def direct_copies(k, d, sender):
@@ -352,7 +351,7 @@
                 copy().start()
 
     def stage_second(k):
-        firsts, seconds = first_copies(k), second_copies(k)
+        seconds = second_copies(k)
         for n, (p, t, r, to, half) in enumerate(
             [
                 (pa, ta2, ra1, xp, 0),
@@ -366,7 +365,8 @@
             @pl.when(k != n % 2)
             def _(n=n, p=p, t=t, r=r, to=to, half=half, mine=mine, rest=rest):
                 t[k, half, rest] = p[k, to, rest].astype(BF)
-                firsts[n]().wait_recv()
+                if half == 0:
+                    bulk(r.at[k], s1.at[n], r1.at[k, n]).wait_recv()
                 t[k, half, mine] = (p[k, to, mine] + r[k, half].astype(F32)).astype(BF)
                 seconds[n]().start()
 
@@ -375,7 +375,7 @@
 
             @pl.when(k != n)
             def _(n=n, p=p, q=q, t=t, r=r, me=me):
-                bulk(r.at[k], s1.at[2 + n], r1.at[k, 4 + n]).wait_recv()
+                bulk(r.at[k], s1.at[2 + n], r1.at[k, 2 + n]).wait_recv()
                 q[k] = p[k, me] + r[k, 0].astype(F32) + r[k, 1].astype(F32)
                 t[k] = q[k].astype(BF)
                 for d in (2, 1, 3):
@@ -536,7 +536,7 @@
             dma((1,)),
             dma((NZ,)),
             dma((4,)),
-            dma((NZ, 6)),
+            dma((NZ, 4)),
             dma((1,)),
             dma((1,)),
             dma((2,)),

time: 60.5 us -> 60.4 us (level)
  no operation moved by 1% of the time
where the time goes in v5:
time: 60.4 us; the launch traced here: 60.2 us
  Pallas kernels  59.6 us (99%)
  between operations  0.64 us (1%)
    pallas_call x1, Pallas kernels, body(): pl.pallas_call(kernel, out_shape=shapes, in_specs=[anyspace] * 6, out_spe...  58.2 us
    pallas_call x1, Pallas kernels, body(): pl.pallas_call(finish, out_shape=shapes, in_specs=[invm, invm], out_specs...  1.39 us

profile of v5, /device:TPU:1, one launch (start us, length us, event | category | flops | bytes accessed | tf_op | source)
XLA Modules:
  0.0 60.2 jit_solution(584889255473832172)
XLA Ops:
  0.6 58.2 %shard_map.77 = (f32[64,128]{1,0:T(8,128)}, f32[1,128]{1,0:T(1,128)}) custom-call(s32[8]{0:T(128)} %cnt_hbm.1, s32[1,2048]{1,0:T(1,128)} %bitcast.6, bf16[2048,1024]{1,0:T(8,128)(2,1)} %x_hbm.1, bf16[2,40,2048]{2,1,0:T(8,128)(2,1)} %basis_hbm.1, bf16[640,2560]{1,0:T(8,128)(2,1)} %bitcast.5, bf16[64,4,2,2560]{3,2,1,0:T(2,128)(2,1)} %own_hbm.1), custom_call_target="tpu_custom_call" | custom-call | tf_op jit(solution)/shard_map/pallas_call | solution.py:488
  58.8 1.4 %shard_map.78 = (f32[64,128]{1,0:T(8,128)}, f32[1,128]{1,0:T(1,128)}) custom-call(f32[64,128]{1,0:T(8,128)} %get-tuple-element.6.inten, f32[1,128]{1,0:T(1,128)} %get-tuple-element.7.top), custom_call_target="tpu_custom_call" | custom-call | tf_op jit(solution)/shard_map/pallas_call | solution.py:560
